TPU v7x, 256 devices: a whole 4x4x8 slice. The times are simulated.
256 devices in a mesh: occ: 16 (over z_lo, x), vir: 16 (over z_hi, y, core).
Axes of the slice: x: 4, y: 4, z: 8 (z_hi: 2, z_lo: 4; z = z_hi * 4 + z_lo), core: 2. Of those that a mesh axis runs over, the one named last changes fastest.
Arguments:
- b_occ: bfloat16 [64, 768, 2304], P('occ', 'vir'), may hold values from -0.86328125 to 0.86328125
- b_outer: bfloat16 [2, 768, 2304], P(None, 'vir', 'occ'), may hold values from -0.86328125 to 0.86328125
- eps_occ: float32 [64], P('occ'), may hold values from -1.5 to -0.3
- eps_outer: float32 [2], replicated, may hold values from -1.5 to -0.3
- eps_vir: float32 [768], P('vir'), may hold values from 0.2 to 3
Outputs:
- gamma_occ: float32 [64, 768, 2304], P('occ', 'vir')
- gamma_outer: float32 [2, 768, 2304], P(None, 'vir', 'occ')
All inputs are finite; a program needn't handle non-finite values.
Results may differ from a plain program's by a relative error of at most 0.0018.
Values may be sent and summed in bfloat16 or wider, within the bound.
No kernel may reach another device: no remote copies, remote signals or barrier semaphores. Data moves between devices by JAX's collectives and lax.ppermute only.
A program may use at most 128 MiB of HBM per device.

v0:
```python
import jax
import jax.numpy as jnp
from jax import lax
from jax.sharding import PartitionSpec as P


def in_order(tiles, dim):
    shape = list(tiles.shape[1:])
    shape[dim] *= tiles.shape[0]
    return jnp.moveaxis(tiles, 0, dim).reshape(shape)


def from_everyone(array, axis):
    devices = lax.axis_size(axis)
    return lax.all_to_all(
        jnp.broadcast_to(array[None], (devices, *array.shape)), axis, 0, 0, tiled=True
    )


def collect(array, axis, dim):
    return in_order(from_everyone(array, axis), dim)


def cut_along(array, dim, devices):
    shape = array.shape
    tiles = array.reshape(*shape[:dim], devices, shape[dim] // devices, *shape[dim + 1 :])
    return jnp.moveaxis(tiles, dim, 0)


def sum_at_owner(array, axis, dim):
    tiles = cut_along(array, dim, lax.axis_size(axis))
    arrived = lax.all_to_all(tiles, axis, split_axis=0, concat_axis=0, tiled=True)
    return arrived.sum(axis=0)


def on_device(b_occ, b_outer, eps_occ, eps_outer, eps_vir):
    aux_full = collect(b_outer, "occ", 2)
    b_whole, eps_whole = (
        lax.all_gather(aux_full, "vir", axis=1, tiled=True),
        lax.all_gather(eps_vir.astype(jnp.bfloat16), "vir", axis=0, tiled=True).astype(
            eps_vir.dtype
        ),
    )
    integral = jnp.einsum("iaq,jbq->ijab", b_occ, b_whole, preferred_element_type=jnp.float32)
    denom = (
        eps_occ[:, None, None, None]
        + eps_outer[None, :, None, None]
        - eps_vir[None, None, :, None]
        - eps_whole[None, None, None, :]
    )
    amps = integral / denom
    received = lax.all_to_all(amps, "vir", split_axis=3, concat_axis=2, tiled=True)
    swapped = jnp.swapaxes(received, 2, 3)
    tilde = 2.0 * amps - swapped
    whole_wide = b_whole.astype(jnp.float32)
    occ_wide = b_occ.astype(jnp.float32)
    gamma_occ = jnp.einsum("ijab,jbq->iaq", tilde, whole_wide, precision=lax.Precision.HIGHEST)
    partial_terms = jnp.einsum("ijab,iaq->jbq", tilde, occ_wide, precision=lax.Precision.HIGHEST)
    section = lax.psum_scatter(partial_terms, "occ", scatter_dimension=2, tiled=True)
    gamma_outer = sum_at_owner(section, "vir", 1)
    return (gamma_occ, gamma_outer)


def solution(mesh):
    placed = (P("occ", "vir", None), P(None, "vir", "occ"), P("occ"), P(), P("vir"))
    return jax.shard_map(
        on_device,
        mesh=mesh,
        in_specs=placed,
        out_specs=(P("occ", "vir", None), P(None, "vir", "occ")),
        check_vma=False,
    )
```

profile of v0, /device:TPU:57, one launch (start us, length us, event | category | flops | bytes accessed | tf_op | source)
XLA Modules:
  0.0 437.4 jit_solution(1682618729027701697)
XLA Ops:
  7.2 0.9 broadcast_in_dim.2
  8.2 27.7 %all_to_all.28 = bf16[16,2,48,144]{3,2,1,0:T(8,128)(2,1)S(1)} all-to-all(bf16[16,2,48,144]{3,2,1,0:T(8,128)(2,1)S(1)} %broadcast_in_dim.2), channel_id=1, replica_groups=mesh['occ'=16,'vir'=16] {'occ'}, dimensions={0} | all-to-all | bytes 884736 | tf_op jit(solution)/shard_map/all_to_all | solution.py:15
  35.8 0.4 copy.12
  36.3 1.9 reshape.51
  38.3 0.6 dynamic-slice
  39.8 44.7 %all-reduce = bf16[768]{0:T(1024)(128)(2,1)S(1)} all-reduce(bf16[768]{0:T(1024)(128)(2,1)S(1)} %dynamic-update-slice), channel_id=1, replica_groups=mesh['occ'=16,'vir'=16] {'vir'}, use_global_device_ids=true, to_apply=%add | all-reduce | flops 768 | bytes 3072
  84.6 51.1 %all-gather.2.cloned.1.call-done = bf16[2,768,2304]{2,1,0:T(8,128)(2,1)} async-done(((bf16[2,48,2304]{2,1,0:T(8,128)(2,1)}), bf16[2,768,2304]{2,1,0:T(8,128)(2,1)}) %all-gather.2.cloned.1.call-update) | async-done | bytes 7077904 | tf_op jit(solution)/shard_map/all_gather | solution.py:39
  135.7 5.4 %fusion.10 = f32[4,2,48,768]{3,2,0,1:T(8,128)S(1)} fusion(bf16[2,768,2304]{2,1,0:T(8,128)(2,1)} %all-gather.2.cloned.1.call-done, bf16[4,48,2304]{2,1,0:T(8,128)(2,1)S(1)} %copy-done, f32[768]{0:T(1024)S(1)} %convert_element_type.9, f32[4,2,48]{2,0,1:T(4,128)S(1)} %broadcast_subtract_fusion), kind=kOutput, calls=%fused_computation.8 | convolution fusion | flops 1359544320 | bytes 9146880 | tf_op jit(solution)/shard_map/iaq,jbq->ijab/dot_general | solution.py:44
  141.1 2.7 copy.13
  143.9 5.7 %reshape.62 = f32[16,1,18432]{2,1,0:T(1,128)} reshape(f32[768,2,4,48]{3,2,1,0:T(4,128)} %bitcast.50) | data formatting | bytes 2359296
  149.6 35.7 %all_to_all.29 = f32[16,1,18432]{2,1,0:T(1,128)S(1)} all-to-all(f32[16,1,18432]{2,1,0:T(1,128)} %reshape.62), channel_id=1, replica_groups=mesh['occ'=16,'vir'=16] {'vir'}, dimensions={0} | all-to-all | bytes 2359296 | tf_op jit(solution)/shard_map/all_to_all | solution.py:52
  185.3 0.5 broadcast.39
  185.9 4.8 %reduce = f32[16,18432]{1,0:T(8,128)} reduce(f32[16,1,18432]{2,1,0:T(1,128)S(1)} %all_to_all.29, f32[]{:T(128)} %broadcast.39), dimensions={1}, to_apply=%all_to_all.20.reduce_sub_computation | reduce | bytes 2359300 | tf_op jit(solution)/shard_map/all_to_all | solution.py:52
  190.6 5.4 %reshape.63 = f32[768,2,4,48]{3,2,1,0:T(4,128)} reshape(f32[16,18432]{1,0:T(8,128)} %reduce) | data formatting | bytes 2359296
  196.0 5.4 %copy.20 = f32[4,2,48,16,48]{2,3,4,0,1:T(8,128)} copy(f32[4,2,48,16,48]{2,0,1,4,3:T(4,128)} %bitcast.48) | data formatting | bytes 2359296 | tf_op jit(solution)/shard_map/all_to_all | solution.py:52
  201.4 2.8 all_to_all.23
  204.2 9.0 %convolution_bitcast_fusion = f32[2,768,2304]{1,2,0:T(8,128)} fusion(bf16[4,48,2304]{2,1,0:T(8,128)(2,1)S(1)} %copy-done, f32[4,2,768,48]{2,3,0,1:T(8,128)S(1)} %all_to_all.23, f32[4,2,48,768]{3,2,0,1:T(8,128)S(1)} %fusion.10), kind=kOutput, calls=%fused_computation | convolution fusion | flops 8154316800 | bytes 17399808 | tf_op jit(solution)/shard_map/ijab,iaq->jbq/dot_general | solution.py:58
  213.3 156.7 %reduce-scatter.2.cloned.1.call-done = f32[2,768,144]{1,2,0:T(8,128)} async-done(((f32[2,768,2304]{1,2,0:T(8,128)}), f32[2,768,144]{1,2,0:T(8,128)}) %reduce-scatter.2.cloned.1.call-update) | async-done | bytes 884752 | tf_op jit(solution)/shard_map/reduce_scatter | solution.py:59
  370.0 2.8 copy.15
  372.8 2.7 copy.16
  375.5 10.3 %all-to-all-start.2 = ((f32[16,2,48,144]{3,2,1,0:T(8,128)}), f32[16,2,48,144]{3,2,1,0:T(8,128)}, u32[]{:S(2)}, u32[]{:S(2)}) async-start(f32[16,2,48,144]{3,2,1,0:T(8,128)} %copy.16), calls=%async_computation.3 | async-start | bytes 3145728 | tf_op jit(solution)/shard_map/all_to_all | solution.py:32
  385.8 7.7 %fusion.4 = f32[4,48,2304]{2,1,0:T(8,128)} fusion(bf16[2,768,2304]{2,1,0:T(8,128)(2,1)} %all-gather.2.cloned.1.call-done, f32[4,2,768,48]{2,3,0,1:T(8,128)S(1)} %all_to_all.23, f32[4,2,48,768]{3,2,0,1:T(8,128)S(1)} %fusion.10), kind=kOutput, calls=%fused_computation.5 | convolution fusion | flops 8154316800 | bytes 11206656 | tf_op jit(solution)/shard_map/ijab,jbq->iaq/dot_general | solution.py:57
  393.5 34.9 %all-to-all-done.2 = f32[16,2,48,144]{3,2,1,0:T(8,128)} async-done(((f32[16,2,48,144]{3,2,1,0:T(8,128)}), f32[16,2,48,144]{3,2,1,0:T(8,128)}, u32[]{:S(2)}, u32[]{:S(2)}) %all-to-all-start.2) | async-done | bytes 884768 | tf_op jit(solution)/shard_map/all_to_all | solution.py:32
  428.4 2.2 reduce_sum.9
  (20 shorter events, 0.5 us)
Async XLA Ops:
  7.2 128.5 %copy-start = (bf16[4,48,2304]{2,1,0:T(8,128)(2,1)S(1)}, bf16[4,48,2304]{2,1,0:T(8,128)(2,1)}, u32[]{:S(2)}) copy-start(bf16[4,48,2304]{2,1,0:T(8,128)(2,1)} %param.5) | copy-start | bytes 2654212
  7.2 128.5 %all-gather.2.cloned.1.call-start = ((), (), s32[]{:S(2)}) async-start(), calls=%async_computation.4 | async-start | bytes 7520256 | tf_op jit(solution)/shard_map/all_gather | solution.py:39
  36.3 2.0 copy-start.3
  36.3 2.0 copy-start.4
  36.3 48.2 %copy-start.1 = (f32[4]{0:T(128)S(1)}, f32[4]{0:T(128)}, u32[]{:S(2)}) copy-start(f32[4]{0:T(128)} %param.7) | copy-start | bytes 52
  36.3 48.2 %copy-start.2 = (f32[2]{0:T(128)S(1)}, f32[2]{0:T(128)}, u32[]{:S(2)}) copy-start(f32[2]{0:T(128)} %param.8) | copy-start | bytes 28
  38.2 331.8 %reduce-scatter.2.cloned.1.call-start = ((), (), s32[]{:S(2)}) async-start(), calls=%async_computation.5 | async-start | bytes 15040512 | tf_op jit(solution)/shard_map/reduce_scatter | solution.py:59
  375.5 53.0 %all-to-all-start.2 = ((f32[16,2,48,144]{3,2,1,0:T(8,128)}), f32[16,2,48,144]{3,2,1,0:T(8,128)}, u32[]{:S(2)}, u32[]{:S(2)}) async-start(f32[16,2,48,144]{3,2,1,0:T(8,128)} %copy.16), calls=%async_computation.3 | async-start | bytes 3145728 | tf_op jit(solution)/shard_map/all_to_all | solution.py:32
Sparse Core Ops, SparseCore 0:
  38.3 97.3 all-gather.1
  213.4 156.5 reduce-scatter.1
where the time goes:
time: 438 us; the launch traced here: 437 us
  waiting for transfers between devices  243 us (55%)
  blocking collectives  108 us (25%)
  local copies, waits for them, and re-layouts  32.1 us (7%)
  matrix products  22.2 us (5%)
  between operations  14.8 us (3%)
  starting transfers between devices  10.4 us (2%)
  other arithmetic  7.1 us (2%)
    reduce_scatter x1, waiting for transfers between devices, on_device(): lax.psum_scatter(partial_terms, 'occ', scatter_dimension=2, tiled=True)  157 us
    all_gather x1, waiting for transfers between devices, on_device(): lax.all_gather(aux_full, 'vir', axis=1, tiled=True)  51.1 us
    unnamed x1, blocking collectives  44.7 us
    all_to_all x1, blocking collectives, on_device(): lax.all_to_all(amps, 'vir', split_axis=3, concat_axis=2, tiled=True)  35.7 us
    all_to_all x1, waiting for transfers between devices, sum_at_owner(): lax.all_to_all(tiles, axis, split_axis=0, concat_axis=0, tiled=True)  34.9 us
    all_to_all x1, blocking collectives, from_everyone(): lax.all_to_all(jnp.broadcast_to(array[None], (devices, *array.shape)), ax...  27.7 us
    unnamed x15, local copies, waits for them, and re-layouts  12 us
    all_to_all x1, starting transfers between devices, sum_at_owner(): lax.all_to_all(tiles, axis, split_axis=0, concat_axis=0, tiled=True)  10.3 us
  transfers between devices with their start and end apart: 3, of which 3 were waited for; matrix products, arithmetic and copies ran while one was open for 2% of the time, Pallas kernels for 0%

commit v1 on v0

--- a/solution.py
+++ b/solution.py
@@ -2,6 +2,11 @@
 import jax.numpy as jnp
 from jax import lax
 from jax.sharding import PartitionSpec as P
+
+
+def all_by_exchange(shard, name, along):
+    sent = jnp.stack([shard] * lax.axis_size(name))
+    return jnp.concatenate(lax.all_to_all(sent, name, 0, 0), axis=along)
 
 
 def in_order(tiles, dim):
@@ -36,7 +41,7 @@
 def on_device(b_occ, b_outer, eps_occ, eps_outer, eps_vir):
     aux_full = collect(b_outer, "occ", 2)
     b_whole, eps_whole = (
-        lax.all_gather(aux_full, "vir", axis=1, tiled=True),
+        all_by_exchange(aux_full, "vir", 1),
         lax.all_gather(eps_vir.astype(jnp.bfloat16), "vir", axis=0, tiled=True).astype(
             eps_vir.dtype
         ),

time: 438 us -> 556 us (1.27)
  blocking collectives: 108 us -> 264 us
  waiting for transfers between devices: 243 us -> 188 us
  starting transfers between devices: 10.4 us -> 20.6 us
  local copies, waits for them, and re-layouts: 32.1 us -> 41.3 us
    unnamed x1, blocking collectives: 44.7 us -> 204 us
    all_gather x1 -> x0, waiting for transfers between devices: 51.1 us -> none  [on_device(): lax.all_gather(aux_full, 'vir', axis=1, tiled=True)]
    all_to_all x0 -> x1, starting transfers between devices: none -> 10.3 us  [all_by_exchange(): return jnp.concatenate(lax.all_to_all(sent, name, 0, 0), axis=along)]
    unnamed x15 -> x17, local copies, waits for them, and re-layouts: 12 us -> 14.8 us
  transfers between devices with their start and end apart: 3 -> 3, of which waited for: 3 -> 2; matrix products, arithmetic and copies ran while one was open for 2% -> 2% of each run, Pallas kernels for 0% -> 0%
where the time goes in v1:
time: 556 us; the launch traced here: 555 us
  blocking collectives  264 us (47%)
  waiting for transfers between devices  188 us (34%)
  local copies, waits for them, and re-layouts  41.3 us (7%)
  starting transfers between devices  20.6 us (4%)
  matrix products  19.2 us (3%)
  between operations  14.8 us (3%)
  other arithmetic  7.1 us (1%)
    unnamed x1, blocking collectives  204 us
    reduce_scatter x1, waiting for transfers between devices, on_device(): lax.psum_scatter(partial_terms, 'occ', scatter_dimension=2, tiled=True)  153 us
    all_to_all x1, waiting for transfers between devices, sum_at_owner(): lax.all_to_all(tiles, axis, split_axis=0, concat_axis=0, tiled=True)  35.1 us
    all_to_all x1, blocking collectives, on_device(): lax.all_to_all(amps, 'vir', split_axis=3, concat_axis=2, tiled=True)  33 us
    all_to_all x1, blocking collectives, from_everyone(): lax.all_to_all(jnp.broadcast_to(array[None], (devices, *array.shape)), ax...  27.7 us
    unnamed x17, local copies, waits for them, and re-layouts  14.8 us
  transfers between devices with their start and end apart: 3, of which 2 were waited for; matrix products, arithmetic and copies ran while one was open for 2% of the time, Pallas kernels for 0%

profile of v1, /device:TPU:57, one launch (start us, length us, event | category | flops | bytes accessed | tf_op | source)
XLA Modules:
  0.0 555.4 jit_solution(16944449736523267549)
XLA Ops:
  7.2 0.9 broadcast_in_dim.2
  8.1 27.7 %all_to_all.33 = bf16[16,2,48,144]{3,2,1,0:T(8,128)(2,1)S(1)} all-to-all(bf16[16,2,48,144]{3,2,1,0:T(8,128)(2,1)S(1)} %broadcast_in_dim.2), channel_id=1, replica_groups=mesh['occ'=16,'vir'=16] {'occ'}, dimensions={0} | all-to-all | bytes 884736 | tf_op jit(solution)/shard_map/all_to_all | solution.py:20
  36.2 1.1 stack_reshape.2
  37.3 3.6 stack.3
  41.0 10.3 %all-to-all-start.1 = ((bf16[16,2,48,2304]{3,2,1,0:T(8,128)(2,1)}), bf16[16,2,48,2304]{3,2,1,0:T(8,128)(2,1)}, u32[]{:S(2)}, u32[]{:S(2)}) async-start(bf16[16,2,48,2304]{3,2,1,0:T(8,128)(2,1)} %stack.3), calls=%async_computation.1 | async-start | bytes 14155776 | tf_op jit(solution)/shard_map/all_to_all | solution.py:9
  52.8 203.8 %all-reduce = bf16[768]{0:T(1024)(128)(2,1)S(1)} all-reduce(bf16[768]{0:T(1024)(128)(2,1)S(1)} %dynamic-update-slice), channel_id=1, replica_groups=mesh['occ'=16,'vir'=16] {'vir'}, use_global_device_ids=true, to_apply=%add | all-reduce | flops 768 | bytes 3072
  256.8 3.5 copy.18
  260.3 2.8 copy-done.1
  263.1 2.4 fusion
  265.5 2.7 copy.19
  268.3 5.7 %reshape.68 = f32[16,1,18432]{2,1,0:T(1,128)} reshape(f32[768,2,4,48]{3,2,1,0:T(4,128)} %bitcast.47) | data formatting | bytes 2359296
  274.0 33.0 %all_to_all.34 = f32[16,1,18432]{2,1,0:T(1,128)S(1)} all-to-all(f32[16,1,18432]{2,1,0:T(1,128)} %reshape.68), channel_id=1, replica_groups=mesh['occ'=16,'vir'=16] {'vir'}, dimensions={0} | all-to-all | bytes 2359296 | tf_op jit(solution)/shard_map/all_to_all | solution.py:57
  307.5 4.8 reduce
  312.3 5.4 reshape.69
  317.7 5.4 copy.26
  323.1 2.8 all_to_all.27
  325.9 9.0 %convolution_bitcast_fusion = f32[2,768,2304]{1,2,0:T(8,128)} fusion(bf16[4,48,2304]{2,1,0:T(8,128)(2,1)S(1)} %copy-done, f32[4,2,768,48]{2,3,0,1:T(8,128)S(1)} %all_to_all.27, f32[4,2,48,768]{3,2,0,1:T(8,128)S(1)} %fusion), kind=kOutput, calls=%fused_computation | convolution fusion | flops 8154316800 | bytes 17399808 | tf_op jit(solution)/shard_map/ijab,iaq->jbq/dot_general | solution.py:63
  334.9 152.8 %reduce-scatter.2.cloned.1.call-done = f32[2,768,144]{1,2,0:T(8,128)} async-done(((f32[2,768,2304]{1,2,0:T(8,128)}), f32[2,768,144]{1,2,0:T(8,128)}) %reduce-scatter.2.cloned.1.call-update) | async-done | bytes 884752 | tf_op jit(solution)/shard_map/reduce_scatter | solution.py:64
  487.8 2.8 copy.21
  490.6 2.7 copy.22
  493.3 10.3 %all-to-all-start.3 = ((f32[16,2,48,144]{3,2,1,0:T(8,128)}), f32[16,2,48,144]{3,2,1,0:T(8,128)}, u32[]{:S(2)}, u32[]{:S(2)}) async-start(f32[16,2,48,144]{3,2,1,0:T(8,128)} %copy.22), calls=%async_computation.4 | async-start | bytes 3145728 | tf_op jit(solution)/shard_map/all_to_all | solution.py:37
  503.6 7.7 %convolution_bitcast_fusion.1 = f32[4,48,2304]{2,1,0:T(8,128)} fusion(bf16[2,768,2304,1]{2,1,3,0:T(8,128)(2,1)} %bitcast.44, f32[4,2,768,48]{2,3,0,1:T(8,128)S(1)} %all_to_all.27, f32[4,2,48,768]{3,2,0,1:T(8,128)S(1)} %fusion), kind=kOutput, calls=%fused_computation.1 | convolution fusion | flops 8154316800 | bytes 11206656 | tf_op jit(solution)/shard_map/ijab,jbq->iaq/dot_general | solution.py:62
  511.3 35.1 %all-to-all-done.3 = f32[16,2,48,144]{3,2,1,0:T(8,128)} async-done(((f32[16,2,48,144]{3,2,1,0:T(8,128)}), f32[16,2,48,144]{3,2,1,0:T(8,128)}, u32[]{:S(2)}, u32[]{:S(2)}) %all-to-all-start.3) | async-done | bytes 884768 | tf_op jit(solution)/shard_map/all_to_all | solution.py:37
  546.4 2.2 reduce_sum.9
  (23 shorter events, 2.0 us)
Async XLA Ops:
  7.2 255.9 %copy-start = (bf16[4,48,2304]{2,1,0:T(8,128)(2,1)S(1)}, bf16[4,48,2304]{2,1,0:T(8,128)(2,1)}, u32[]{:S(2)}) copy-start(bf16[4,48,2304]{2,1,0:T(8,128)(2,1)} %param.5) | copy-start | bytes 2654212
  41.0 10.3 %copy-start.4 = (f32[48]{0:T(128)S(1)}, f32[48]{0:T(128)}, u32[]{:S(2)}) copy-start(f32[48]{0:T(128)} %param.9) | copy-start | bytes 580
  41.0 10.3 %copy-start.5 = (u32[256]{0:T(256)S(1)}, u32[256]{0:T(256)}, u32[]{:S(2)}) copy-start(u32[256]{0:T(256)} %constant.8) | copy-start | bytes 3076
  41.0 215.7 %copy-start.2 = (f32[4]{0:T(128)S(1)}, f32[4]{0:T(128)}, u32[]{:S(2)}) copy-start(f32[4]{0:T(128)} %param.7) | copy-start | bytes 52
  41.0 215.7 %copy-start.3 = (f32[2]{0:T(128)S(1)}, f32[2]{0:T(128)}, u32[]{:S(2)}) copy-start(f32[2]{0:T(128)} %param.8) | copy-start | bytes 28
  41.0 215.8 %all-to-all-start.1 = ((bf16[16,2,48,2304]{3,2,1,0:T(8,128)(2,1)}), bf16[16,2,48,2304]{3,2,1,0:T(8,128)(2,1)}, u32[]{:S(2)}, u32[]{:S(2)}) async-start(bf16[16,2,48,2304]{3,2,1,0:T(8,128)(2,1)} %stack.3), calls=%async_computation.1 | async-start | bytes 14155776 | tf_op jit(solution)/shard_map/all_to_all | solution.py:9
  51.2 436.6 %reduce-scatter.2.cloned.1.call-start = ((), (), s32[]{:S(2)}) async-start(), calls=%async_computation.5 | async-start | bytes 15040512 | tf_op jit(solution)/shard_map/reduce_scatter | solution.py:64
  260.3 2.8 copy-start.1
  493.3 53.1 %all-to-all-start.3 = ((f32[16,2,48,144]{3,2,1,0:T(8,128)}), f32[16,2,48,144]{3,2,1,0:T(8,128)}, u32[]{:S(2)}, u32[]{:S(2)}) async-start(f32[16,2,48,144]{3,2,1,0:T(8,128)} %copy.22), calls=%async_computation.4 | async-start | bytes 3145728 | tf_op jit(solution)/shard_map/all_to_all | solution.py:37
Sparse Core Ops, SparseCore 0:
  335.1 152.6 reduce-scatter.1
